TPU v7x, 32 devices: a whole 2x2x4 slice. The times are simulated.
32 devices in a mesh: gx: 2 (over y), gy: 4 (over x, core), gz: 4 (over z).
Axes of the slice: x: 2, y: 2, z: 4, core: 2. Of those that a mesh axis runs over, the one named last changes fastest.
Arguments:
- volume: float32 [16, 64, 512], P(('gx', 'gy'), None, 'gz'), may hold values from 0 to 1
- levels: int32 [4], replicated, may hold values from 0 to 255
Outputs:
- labelling: float32 [4, 16, 64, 512], P(None, 'gx', 'gy', 'gz')
- centers: float32 [4], replicated
All inputs are finite; a program needn't handle non-finite values.
Results may differ from a plain program's by a relative error of at most 0.0001.
Values sent between devices are 32-bit elements; how exact they have to be, the bound alone decides.
A program may use at most 64 MiB of HBM per device.

v0:
```python
import jax
import jax.numpy as jnp
from jax import lax
from jax.sharding import PartitionSpec as P

ITERS = 2
tau_step = 0.25
sigma_step = 0.25
smooth_weight = 0.5
prior_weight = 1.0


def with_halo(block, sides, width):
    for axis, dim in sides:
        count = lax.axis_size(axis)
        forward = [(i, i + 1) for i in range(count - 1)]
        backward = [(target, source) for source, target in forward]
        low = lax.ppermute(
            lax.slice_in_dim(block, block.shape[dim] - width, None, axis=dim), axis, forward
        )
        high = lax.ppermute(lax.slice_in_dim(block, 0, width, axis=dim), axis, backward)
        block = jnp.concatenate([low, block, high], axis=dim)
    return block


def project_simplex(values):
    how_many = values.shape[0]
    threshold = None
    for subset in range(1, 1 << how_many):
        members = [label_index for label_index in range(how_many) if subset >> label_index & 1]
        summed = values[members[0]]
        for label_index in members[1:]:
            summed = summed + values[label_index]
        candidate = (summed - 1.0) / float(len(members))
        threshold = candidate if threshold is None else jnp.maximum(threshold, candidate)
    return jnp.maximum(values - threshold[None], 0.0)


def bounds(start, total, extent):
    position = start - 1 + jnp.arange(extent + 1, dtype=jnp.int32)
    return (position >= 0, position < total - 1)


def local(volume, levels):
    thickness = volume.shape[0]
    x_start = (lax.axis_index("gx") * lax.axis_size("gy") + lax.axis_index("gy")) * thickness
    x_total = thickness * lax.axis_size("gx") * lax.axis_size("gy")
    y_start = 0
    y_total = volume.shape[1]
    z_start = lax.axis_index("gz") * volume.shape[2]
    z_total = volume.shape[2] * lax.axis_size("gz")
    extent = volume.shape
    how_many = levels.shape[0]
    inside_x, ahead_x = bounds(x_start, x_total, extent[0])
    inside_y, ahead_y = bounds(y_start, y_total, extent[1])
    inside_z, ahead_z = bounds(z_start, z_total, extent[2])
    inside = (inside_x[:, None, None] & inside_y[None, :, None] & inside_z[None, None, :]).astype(
        jnp.float32
    )
    base_levels = levels.astype(jnp.float32) / 255.0
    centers = base_levels
    starting = (volume[None] - base_levels[:, None, None, None]) ** 2
    labelling = project_simplex(1.0 / how_many - tau_step * starting)
    smoothed = labelling
    dual_field = jnp.zeros((how_many, 3, extent[0] + 1, extent[1] + 1, extent[2] + 1), jnp.float32)
    for iteration in range(ITERS):
        padded = with_halo(smoothed, ((("gx", "gy"), 1), ("gz", 3)), 1)
        padded = jnp.pad(padded, ((0, 0), (0, 0), (1, 1), (0, 0)))
        corner = padded[:, :-1, :-1, :-1]
        grad_x = jnp.where(ahead_x[:, None, None], padded[:, 1:, :-1, :-1] - corner, 0.0)
        grad_y = jnp.where(ahead_y[None, :, None], padded[:, :-1, 1:, :-1] - corner, 0.0)
        grad_z = jnp.where(ahead_z[None, None, :], padded[:, :-1, :-1, 1:] - corner, 0.0)
        stepped = dual_field + sigma_step * jnp.stack([grad_x, grad_y, grad_z], axis=1)
        length = jnp.sqrt(
            stepped[:, 0] * stepped[:, 0]
            + stepped[:, 1] * stepped[:, 1]
            + stepped[:, 2] * stepped[:, 2]
        )
        shrink = inside / jnp.maximum(1.0, length / smooth_weight)
        dual_field = stepped * shrink[:, None]
        divergence = (
            dual_field[:, 0, 1:, 1:, 1:]
            - dual_field[:, 0, :-1, 1:, 1:]
            + (dual_field[:, 1, 1:, 1:, 1:] - dual_field[:, 1, 1:, :-1, 1:])
            + (dual_field[:, 2, 1:, 1:, 1:] - dual_field[:, 2, 1:, 1:, :-1])
        )
        fidelity = (volume[None] - centers[:, None, None, None]) ** 2
        updated = project_simplex(labelling + tau_step * (divergence - fidelity))
        smoothed = 2.0 * updated - labelling
        labelling = updated
        sizes_local = jnp.sum(labelling, axis=(1, 2, 3))
        weighted = jnp.sum(labelling * volume[None], axis=(1, 2, 3))
        sizes_all, weighted_all = lax.psum((sizes_local, weighted), ("gx", "gy", "gz"))
        centers = (weighted_all + prior_weight * base_levels) / (sizes_all + prior_weight)
    labelling = lax.all_to_all(labelling, "gy", split_axis=2, concat_axis=1, tiled=True)
    return (labelling, centers)


def solution(mesh):
    return jax.shard_map(
        local,
        mesh=mesh,
        in_specs=(P(("gx", "gy"), None, "gz"), P()),
        out_specs=(P(None, "gx", "gy", "gz"), P()),
        check_vma=False,
    )
```

profile of v0, /device:TPU:0, one launch (start us, length us, event | category | flops | bytes accessed | tf_op | source)
XLA Modules:
  0.0 159.2 jit_solution(3588290688517704985)
XLA Ops:
  0.6 0.7 convert_multiply_fusion
  1.3 0.9 multiply_subtract_fusion.1
  2.2 0.1 maximum_bitcast_fusion.2
  2.4 0.6 copy-done.8
  3.0 1.0 subtract_maximum_fusion.2
  4.0 2.4 %collective-permute-start = (f32[4,1,64,128]{3,2,1,0:T(8,128)S(1)}, f32[4,1,64,128]{3,2,1,0:T(8,128)S(1)}, u32[]{:S(2)}, u32[]{:S(2)}) collective-permute-start(f32[4,1,64,128]{3,2,1,0:T(8,128)S(1)} %get-tuple-element.24), channel_id=1, source_target_pairs={{0,4},{4,8},{8,12},{12,16},{16,20},{20,24},{24,28},{1,5},{5,9},{9,... | collective-permute-start | bytes 393224 | tf_op jit(solution)/shard_map/ppermute | solution.py:18
  6.4 1.3 collective-permute-start.1
  7.7 0.1 broadcast_and_fusion
  7.8 0.1 and_convert_fusion
  8.0 0.0 collective-permute-done
  8.0 3.7 %collective-permute-done.1 = f32[4,1,64,128]{3,2,1,0:T(8,128)S(1)} collective-permute-done((f32[4,1,64,128]{3,2,1,0:T(8,128)S(1)}, f32[4,1,64,128]{3,2,1,0:T(8,128)S(1)}, u32[]{:S(2)}, u32[]{:S(2)}) %collective-permute-start.1) | collective-permute-done | bytes 131104 | tf_op jit(solution)/shard_map/ppermute | solution.py:21
  11.8 0.2 fusion.66
  12.0 3.5 %collective-permute-start.2 = (f32[4,4,64,1]{3,2,1,0:T(8,128)S(1)}, f32[4,4,64,1]{3,2,1,0:T(8,128)S(1)}, u32[]{:S(2)}, u32[]{:S(2)}) collective-permute-start(f32[4,4,64,1]{3,2,1,0:T(8,128)S(1)} %get-tuple-element.19), channel_id=1, source_target_pairs={{0,1},{1,2},{2,3},{4,5},{5,6},{6,7},{8,9},{9,10},{10,11},{12,13},{... | collective-permute-start | bytes 12296 | tf_op jit(solution)/shard_map/ppermute | solution.py:18
  15.5 1.3 collective-permute-start.3
  16.8 8.4 %collective-permute-done.2 = f32[4,4,64,1]{3,2,1,0:T(8,128)S(1)} collective-permute-done((f32[4,4,64,1]{3,2,1,0:T(8,128)S(1)}, f32[4,4,64,1]{3,2,1,0:T(8,128)S(1)}, u32[]{:S(2)}, u32[]{:S(2)}) %collective-permute-start.2) | collective-permute-done | bytes 4128 | tf_op jit(solution)/shard_map/ppermute | solution.py:18
  25.2 4.7 %collective-permute-done.3 = f32[4,4,64,1]{3,2,1,0:T(8,128)S(1)} collective-permute-done((f32[4,4,64,1]{3,2,1,0:T(8,128)S(1)}, f32[4,4,64,1]{3,2,1,0:T(8,128)S(1)}, u32[]{:S(2)}, u32[]{:S(2)}) %collective-permute-start.3) | collective-permute-done | bytes 4128 | tf_op jit(solution)/shard_map/ppermute | solution.py:21
  29.9 0.5 select_maximum_fusion.4
  30.4 0.5 fusion.29
  30.9 0.2 fusion.2
  31.2 0.5 fusion.30
  31.7 0.0 copy-start.4
  31.7 0.0 copy-start.9
  31.7 0.3 fusion.1
  32.0 0.5 copy-done.4
  32.5 0.0 copy-done.9
  32.6 0.5 fusion.41
  33.0 0.1 maximum_bitcast_fusion.1
  33.1 0.9 copy-done
  34.1 1.1 multiply_reduce_fusion.1
  35.2 0.7 copy-done.2
  35.9 0.7 fusion.67
  36.6 4.7 %collective-permute-start.4 = (f32[4,1,64,128]{3,2,1,0:T(8,128)}, f32[4,1,64,128]{3,2,1,0:T(8,128)}, u32[]{:S(2)}, u32[]{:S(2)}) collective-permute-start(f32[4,1,64,128]{3,2,1,0:T(8,128)} %get-tuple-element.22), channel_id=1, source_target_pairs={{0,4},{4,8},{8,12},{12,16},{16,20},{20,24},{24,28},{1,5},{5,9},{9,... | collective-permute-start | bytes 393224 | tf_op jit(solution)/shard_map/ppermute | solution.py:18
  41.3 1.3 collective-permute-start.5
  42.6 44.4 %all-reduce.3 = (f32[4]{0:T(128)}, f32[4]{0:T(128)}) all-reduce(f32[4]{0:T(128)} %get-tuple-element.3, f32[4]{0:T(128)} %get-tuple-element.2), channel_id=1, replica_groups=mesh['gx'=2,'gy'=4,'gz'=4] {'gx','gy','gz'}, use_global_device_ids=true, to_apply=%region_3.4 | all-reduce | flops 8 | bytes 64 | tf_op jit(solution)/shard_map/psum | solution.py:93
  87.0 0.0 collective-permute-done.4
  87.0 0.0 collective-permute-done.5
  87.0 1.1 pad_maximum_fusion.2
  88.2 0.2 fusion.65
  88.4 2.3 %collective-permute-start.6 = (f32[4,4,64,1]{3,2,1,0:T(8,128)S(1)}, f32[4,4,64,1]{3,2,1,0:T(8,128)S(1)}, u32[]{:S(2)}, u32[]{:S(2)}) collective-permute-start(f32[4,4,64,1]{3,2,1,0:T(8,128)S(1)} %get-tuple-element.17), channel_id=1, source_target_pairs={{0,1},{1,2},{2,3},{4,5},{5,6},{6,7},{8,9},{9,10},{10,11},{12,13},{... | collective-permute-start | bytes 12296 | tf_op jit(solution)/shard_map/ppermute | solution.py:18
  90.7 1.3 collective-permute-start.7
  92.0 0.0 copy-done.13
  92.0 0.0 copy-done.16
  92.1 0.0 copy-done.17
  92.1 9.2 %collective-permute-done.6 = f32[4,4,64,1]{3,2,1,0:T(8,128)S(1)} collective-permute-done((f32[4,4,64,1]{3,2,1,0:T(8,128)S(1)}, f32[4,4,64,1]{3,2,1,0:T(8,128)S(1)}, u32[]{:S(2)}, u32[]{:S(2)}) %collective-permute-start.6) | collective-permute-done | bytes 4128 | tf_op jit(solution)/shard_map/ppermute | solution.py:18
  101.3 4.1 %collective-permute-done.7 = f32[4,4,64,1]{3,2,1,0:T(8,128)S(1)} collective-permute-done((f32[4,4,64,1]{3,2,1,0:T(8,128)S(1)}, f32[4,4,64,1]{3,2,1,0:T(8,128)S(1)}, u32[]{:S(2)}, u32[]{:S(2)}) %collective-permute-start.7) | collective-permute-done | bytes 4128 | tf_op jit(solution)/shard_map/ppermute | solution.py:21
  105.5 1.5 select_maximum_fusion
  107.0 0.4 fusion.16
  107.4 0.4 fusion
  107.9 0.5 copy-done.7
  108.3 0.5 fusion.9
  108.8 0.0 copy-start.5
  108.8 0.0 copy-start.10
  108.9 0.5 broadcast_multiply_fusion
  109.4 1.2 copy-done.1
  110.6 0.8 fusion.35
  111.4 0.1 maximum_bitcast_fusion
  111.5 0.2 multiply_reduce_fusion
  111.6 0.9 copy.8
  112.5 3.9 %all-to-all-start = ((f32[4,2,64,128]{3,1,0,2:T(2,128)}), f32[4,2,64,128]{3,1,0,2:T(2,128)S(1)}, u32[]{:S(2)}, u32[]{:S(2)}) async-start(f32[4,2,64,128]{3,1,0,2:T(2,128)} %copy.8), calls=%async_computation | async-start | bytes 524288 | tf_op jit(solution)/shard_map/all_to_all | solution.py:95
  116.4 41.5 %all-reduce.2 = (f32[4]{0:T(128)S(1)}, f32[4]{0:T(128)S(1)}) all-reduce(f32[4]{0:T(128)S(1)} %get-tuple-element.5, f32[4]{0:T(128)S(1)} %get-tuple-element.4), channel_id=1, replica_groups=mesh['gx'=2,'gy'=4,'gz'=4] {'gx','gy','gz'}, use_global_device_ids=true, to_apply=%region_7.8 | all-reduce | flops 8 | bytes 64 | tf_op jit(solution)/shard_map/psum | solution.py:93
  157.9 0.5 add_divide_fusion
  158.4 0.0 all-to-all-done
  158.4 0.1 copy.9
  158.5 0.7 copy.10
  (31 shorter events, 0.2 us)
Async XLA Ops:
  2.4 0.6 copy-start.8
  4.0 4.0 %collective-permute-start = (f32[4,1,64,128]{3,2,1,0:T(8,128)S(1)}, f32[4,1,64,128]{3,2,1,0:T(8,128)S(1)}, u32[]{:S(2)}, u32[]{:S(2)}) collective-permute-start(f32[4,1,64,128]{3,2,1,0:T(8,128)S(1)} %get-tuple-element.24), channel_id=1, source_target_pairs={{0,4},{4,8},{8,12},{12,16},{16,20},{20,24},{24,28},{1,5},{5,9},{9,... | collective-permute-start | bytes 393224 | tf_op jit(solution)/shard_map/ppermute | solution.py:18
  6.4 5.3 %collective-permute-start.1 = (f32[4,1,64,128]{3,2,1,0:T(8,128)S(1)}, f32[4,1,64,128]{3,2,1,0:T(8,128)S(1)}, u32[]{:S(2)}, u32[]{:S(2)}) collective-permute-start(f32[4,1,64,128]{3,2,1,0:T(8,128)S(1)} %get-tuple-element.25), channel_id=1, source_target_pairs={{4,0},{8,4},{12,8},{16,12},{20,16},{24,20},{28,24},{5,1},{9,5},{13... | collective-permute-start | bytes 393224 | tf_op jit(solution)/shard_map/ppermute | solution.py:21
  7.9 23.2 %copy-start.6 = (f32[3,65,129]{2,1,0:T(8,128)}, f32[3,65,129]{2,1,0:T(8,128)S(1)}, u32[]{:S(2)}) copy-start(f32[3,65,129]{2,1,0:T(8,128)S(1)} %and_convert_fusion) | copy-start | bytes 301864
  12.0 13.2 %collective-permute-start.2 = (f32[4,4,64,1]{3,2,1,0:T(8,128)S(1)}, f32[4,4,64,1]{3,2,1,0:T(8,128)S(1)}, u32[]{:S(2)}, u32[]{:S(2)}) collective-permute-start(f32[4,4,64,1]{3,2,1,0:T(8,128)S(1)} %get-tuple-element.19), channel_id=1, source_target_pairs={{0,1},{1,2},{2,3},{4,5},{5,6},{6,7},{8,9},{9,10},{10,11},{12,13},{... | collective-permute-start | bytes 12296 | tf_op jit(solution)/shard_map/ppermute | solution.py:18
  15.5 14.4 %collective-permute-start.3 = (f32[4,4,64,1]{3,2,1,0:T(8,128)S(1)}, f32[4,4,64,1]{3,2,1,0:T(8,128)S(1)}, u32[]{:S(2)}, u32[]{:S(2)}) collective-permute-start(f32[4,4,64,1]{3,2,1,0:T(8,128)S(1)} %get-tuple-element.20), channel_id=1, source_target_pairs={{1,0},{2,1},{3,2},{5,4},{6,5},{7,6},{9,8},{10,9},{11,10},{13,12},{... | collective-permute-start | bytes 12296 | tf_op jit(solution)/shard_map/ppermute | solution.py:21
  16.8 14.1 %copy-start.14 = (pred[65]{0:T(512)(128)(4,1)}, pred[65]{0:T(512)(128)(4,1)S(1)}, u32[]{:S(2)}) copy-start(pred[65]{0:T(512)(128)(4,1)S(1)} %fusion.62) | copy-start | bytes 199
  31.7 0.8 copy-start.4
  31.7 0.9 copy-start.9
  32.5 1.5 copy-start
  34.1 2.6 %copy-start.11 = (f32[2,64,128]{2,1,0:T(8,128)}, f32[2,64,128]{2,1,0:T(8,128)S(1)}, u32[]{:S(2)}) copy-start(f32[2,64,128]{2,1,0:T(8,128)S(1)} %maximum_bitcast_fusion.1) | copy-start | bytes 196612
  34.1 58.0 %copy-start.13 = (s32[4]{0:T(128)S(1)}, s32[4]{0:T(128)}, u32[]{:S(2)}) copy-start(s32[4]{0:T(128)} %param.3) | copy-start | bytes 52
  35.2 0.7 copy-start.2
  36.6 50.4 %collective-permute-start.4 = (f32[4,1,64,128]{3,2,1,0:T(8,128)}, f32[4,1,64,128]{3,2,1,0:T(8,128)}, u32[]{:S(2)}, u32[]{:S(2)}) collective-permute-start(f32[4,1,64,128]{3,2,1,0:T(8,128)} %get-tuple-element.22), channel_id=1, source_target_pairs={{0,4},{4,8},{8,12},{12,16},{16,20},{20,24},{24,28},{1,5},{5,9},{9,... | collective-permute-start | bytes 393224 | tf_op jit(solution)/shard_map/ppermute | solution.py:18
  41.3 45.7 %collective-permute-start.5 = (f32[4,1,64,128]{3,2,1,0:T(8,128)}, f32[4,1,64,128]{3,2,1,0:T(8,128)}, u32[]{:S(2)}, u32[]{:S(2)}) collective-permute-start(f32[4,1,64,128]{3,2,1,0:T(8,128)} %get-tuple-element.23), channel_id=1, source_target_pairs={{4,0},{8,4},{12,8},{16,12},{20,16},{24,20},{28,24},{5,1},{9,5},{13... | collective-permute-start | bytes 393224 | tf_op jit(solution)/shard_map/ppermute | solution.py:21
  87.0 5.0 %copy-start.16 = (f32[4]{0:T(128)S(1)}, f32[4]{0:T(128)}, u32[]{:S(2)}) copy-start(f32[4]{0:T(128)} %get-tuple-element.8) | copy-start | bytes 52
  87.0 5.0 %copy-start.17 = (f32[4]{0:T(128)S(1)}, f32[4]{0:T(128)}, u32[]{:S(2)}) copy-start(f32[4]{0:T(128)} %get-tuple-element.9) | copy-start | bytes 52
  87.0 18.4 %copy-start.3 = (f32[4,2,64,128]{3,2,1,0:T(8,128)S(1)}, f32[4,2,64,128]{3,2,1,0:T(8,128)}, u32[]{:S(2)}) copy-start(f32[4,2,64,128]{3,2,1,0:T(8,128)} %copy-done.2) | copy-start | bytes 786436
  88.2 18.8 %copy-start.15 = (pred[65]{0:T(512)(128)(4,1)S(1)}, pred[65]{0:T(512)(128)(4,1)}, u32[]{:S(2)}) copy-start(pred[65]{0:T(512)(128)(4,1)} %copy-done.14) | copy-start | bytes 199
  88.4 12.9 %collective-permute-start.6 = (f32[4,4,64,1]{3,2,1,0:T(8,128)S(1)}, f32[4,4,64,1]{3,2,1,0:T(8,128)S(1)}, u32[]{:S(2)}, u32[]{:S(2)}) collective-permute-start(f32[4,4,64,1]{3,2,1,0:T(8,128)S(1)} %get-tuple-element.17), channel_id=1, source_target_pairs={{0,1},{1,2},{2,3},{4,5},{5,6},{6,7},{8,9},{9,10},{10,11},{12,13},{... | collective-permute-start | bytes 12296 | tf_op jit(solution)/shard_map/ppermute | solution.py:18
  90.7 14.7 %collective-permute-start.7 = (f32[4,4,64,1]{3,2,1,0:T(8,128)S(1)}, f32[4,4,64,1]{3,2,1,0:T(8,128)S(1)}, u32[]{:S(2)}, u32[]{:S(2)}) collective-permute-start(f32[4,4,64,1]{3,2,1,0:T(8,128)S(1)} %get-tuple-element.18), channel_id=1, source_target_pairs={{1,0},{2,1},{3,2},{5,4},{6,5},{7,6},{9,8},{10,9},{11,10},{13,12},{... | collective-permute-start | bytes 12296 | tf_op jit(solution)/shard_map/ppermute | solution.py:21
  107.4 0.9 copy-start.7
  108.8 1.8 %copy-start.1 = (f32[4,3,3,65,129]{4,3,2,0,1:T(8,128)S(1)}, f32[4,3,3,65,129]{4,3,2,0,1:T(8,128)}, u32[]{:S(2)}) copy-start(f32[4,3,3,65,129]{4,3,2,0,1:T(8,128)} %copy-done) | copy-start | bytes 3622324
  108.8 1.7 %copy-start.5 = (f32[2,64,128]{2,1,0:T(8,128)S(1)}, f32[2,64,128]{2,1,0:T(8,128)}, u32[]{:S(2)}) copy-start(f32[2,64,128]{2,1,0:T(8,128)} %param.2) | copy-start | bytes 196612
  108.8 1.7 %copy-start.10 = (f32[2,64,128]{2,1,0:T(8,128)S(1)}, f32[2,64,128]{2,1,0:T(8,128)}, u32[]{:S(2)}) copy-start(f32[2,64,128]{2,1,0:T(8,128)} %copy-done.8) | copy-start | bytes 196612
  108.8 1.7 %copy-start.12 = (f32[2,64,128]{2,1,0:T(8,128)S(1)}, f32[2,64,128]{2,1,0:T(8,128)}, u32[]{:S(2)}) copy-start(f32[2,64,128]{2,1,0:T(8,128)} %copy-done.11) | copy-start | bytes 196612
  112.5 45.9 %all-to-all-start = ((f32[4,2,64,128]{3,1,0,2:T(2,128)}), f32[4,2,64,128]{3,1,0,2:T(2,128)S(1)}, u32[]{:S(2)}, u32[]{:S(2)}) async-start(f32[4,2,64,128]{3,1,0,2:T(2,128)} %copy.8), calls=%async_computation | async-start | bytes 524288 | tf_op jit(solution)/shard_map/all_to_all | solution.py:95
where the time goes:
time: 160 us; the launch traced here: 159 us
  blocking collectives  85.9 us (54%)
  waiting for transfers between devices  30.2 us (19%)
  starting transfers between devices  22 us (14%)
  other arithmetic  12.8 us (8%)
  local copies, waits for them, and re-layouts  7.36 us (5%)
    psum x2, blocking collectives, local(): lax.psum((sizes_local, weighted), ('gx', 'gy', 'gz'))  85.9 us
    ppermute x4, waiting for transfers between devices, with_halo(): lax.ppermute(lax.slice_in_dim(block, block.shape[dim] - width, None, axis...  17.6 us
    ppermute x4, starting transfers between devices, with_halo(): lax.ppermute(lax.slice_in_dim(block, block.shape[dim] - width, None, axis...  12.9 us
    ppermute x4, waiting for transfers between devices, with_halo(): lax.ppermute(lax.slice_in_dim(block, 0, width, axis=dim), axis, backward)  12.6 us
    ppermute x4, starting transfers between devices, with_halo(): lax.ppermute(lax.slice_in_dim(block, 0, width, axis=dim), axis, backward)  5.16 us
    unnamed x36, local copies, waits for them, and re-layouts  4.51 us
    all_to_all x1, starting transfers between devices, local(): lax.all_to_all(labelling, 'gy', split_axis=2, concat_axis=1, tiled=True)  3.9 us
  transfers between devices with their start and end apart: 9, of which 5 were waited for; matrix products, arithmetic and copies ran while one was open for 0% of the time, Pallas kernels for 0%

commit v1 on v0

--- a/solution.py
+++ b/solution.py
@@ -8,6 +8,11 @@
 sigma_step = 0.25
 smooth_weight = 0.5
 prior_weight = 1.0
+
+
+def one_after_other(x, first, second):
+    inner = lax.psum(x, first)
+    return lax.psum(inner, second)
 
 
 def with_halo(block, sides, width):
@@ -90,7 +95,7 @@
         labelling = updated
         sizes_local = jnp.sum(labelling, axis=(1, 2, 3))
         weighted = jnp.sum(labelling * volume[None], axis=(1, 2, 3))
-        sizes_all, weighted_all = lax.psum((sizes_local, weighted), ("gx", "gy", "gz"))
+        sizes_all, weighted_all = one_after_other((sizes_local, weighted), ("gy", "gz"), "gx")
         centers = (weighted_all + prior_weight * base_levels) / (sizes_all + prior_weight)
     labelling = lax.all_to_all(labelling, "gy", split_axis=2, concat_axis=1, tiled=True)
     return (labelling, centers)

time: 160 us -> 149 us (0.931)
  blocking collectives: 85.9 us -> 78.4 us
  waiting for transfers between devices: 30.2 us -> 26.6 us
    psum x2 -> x4, blocking collectives: 85.9 us -> 78.4 us  [the longest x2 67.8 us: one_after_other(): inner = lax.psum(x, first)]
    ppermute x4, waiting for transfers between devices: 17.6 us -> 13.9 us  [with_halo(): lax.ppermute(lax.slice_in_dim(block, block.shape[dim] - width, None, axis...]
  transfers between devices with their start and end apart: 9 -> 9, of which waited for: 5 -> 5; matrix products, arithmetic and copies ran while one was open for 0% -> 1% of each run, Pallas kernels for 0% -> 0%
where the time goes in v1:
time: 149 us; the launch traced here: 148 us
  blocking collectives  78.4 us (53%)
  waiting for transfers between devices  26.6 us (18%)
  starting transfers between devices  21.8 us (15%)
  other arithmetic  12.8 us (9%)
  local copies, waits for them, and re-layouts  7.37 us (5%)
    psum x2, blocking collectives, one_after_other(): inner = lax.psum(x, first)  67.8 us
    ppermute x4, waiting for transfers between devices, with_halo(): lax.ppermute(lax.slice_in_dim(block, block.shape[dim] - width, None, axis...  13.9 us
    ppermute x4, starting transfers between devices, with_halo(): lax.ppermute(lax.slice_in_dim(block, block.shape[dim] - width, None, axis...  13.2 us
    ppermute x4, waiting for transfers between devices, with_halo(): lax.ppermute(lax.slice_in_dim(block, 0, width, axis=dim), axis, backward)  12.7 us
    psum x2, blocking collectives, one_after_other(): return lax.psum(inner, second)  10.5 us
    ppermute x4, starting transfers between devices, with_halo(): lax.ppermute(lax.slice_in_dim(block, 0, width, axis=dim), axis, backward)  5.16 us
    unnamed x36, local copies, waits for them, and re-layouts  4.52 us
    all_to_all x1, starting transfers between devices, local(): lax.all_to_all(labelling, 'gy', split_axis=2, concat_axis=1, tiled=True)  3.41 us
  transfers between devices with their start and end apart: 9, of which 5 were waited for; matrix products, arithmetic and copies ran while one was open for 1% of the time, Pallas kernels for 0%

profile of v1, /device:TPU:0, one launch (start us, length us, event | category | flops | bytes accessed | tf_op | source)
XLA Modules:
  0.0 147.9 jit_solution(13220926109001378380)
XLA Ops:
  0.6 0.7 convert_multiply_fusion
  1.3 0.9 multiply_subtract_fusion.1
  2.2 0.1 maximum_bitcast_fusion.2
  2.4 0.6 copy-done.8
  3.0 1.0 subtract_maximum_fusion.2
  4.0 2.4 %collective-permute-start = (f32[4,1,64,128]{3,2,1,0:T(8,128)S(1)}, f32[4,1,64,128]{3,2,1,0:T(8,128)S(1)}, u32[]{:S(2)}, u32[]{:S(2)}) collective-permute-start(f32[4,1,64,128]{3,2,1,0:T(8,128)S(1)} %get-tuple-element.28), channel_id=1, source_target_pairs={{0,4},{4,8},{8,12},{12,16},{16,20},{20,24},{24,28},{1,5},{5,9},{9,... | collective-permute-start | bytes 393224 | tf_op jit(solution)/shard_map/ppermute | solution.py:23
  6.4 1.3 collective-permute-start.1
  7.8 0.1 broadcast_and_fusion
  7.8 0.1 and_convert_fusion
  8.0 0.0 collective-permute-done
  8.0 3.7 %collective-permute-done.1 = f32[4,1,64,128]{3,2,1,0:T(8,128)S(1)} collective-permute-done((f32[4,1,64,128]{3,2,1,0:T(8,128)S(1)}, f32[4,1,64,128]{3,2,1,0:T(8,128)S(1)}, u32[]{:S(2)}, u32[]{:S(2)}) %collective-permute-start.1) | collective-permute-done | bytes 131104 | tf_op jit(solution)/shard_map/ppermute | solution.py:26
  11.8 0.2 fusion.66
  12.0 3.5 %collective-permute-start.2 = (f32[4,4,64,1]{3,2,1,0:T(8,128)S(1)}, f32[4,4,64,1]{3,2,1,0:T(8,128)S(1)}, u32[]{:S(2)}, u32[]{:S(2)}) collective-permute-start(f32[4,4,64,1]{3,2,1,0:T(8,128)S(1)} %get-tuple-element.23), channel_id=1, source_target_pairs={{0,1},{1,2},{2,3},{4,5},{5,6},{6,7},{8,9},{9,10},{10,11},{12,13},{... | collective-permute-start | bytes 12296 | tf_op jit(solution)/shard_map/ppermute | solution.py:23
  15.5 1.3 collective-permute-start.3
  16.8 0.0 copy-start.14
  16.8 8.4 %collective-permute-done.2 = f32[4,4,64,1]{3,2,1,0:T(8,128)S(1)} collective-permute-done((f32[4,4,64,1]{3,2,1,0:T(8,128)S(1)}, f32[4,4,64,1]{3,2,1,0:T(8,128)S(1)}, u32[]{:S(2)}, u32[]{:S(2)}) %collective-permute-start.2) | collective-permute-done | bytes 4128 | tf_op jit(solution)/shard_map/ppermute | solution.py:23
  25.2 4.7 %collective-permute-done.3 = f32[4,4,64,1]{3,2,1,0:T(8,128)S(1)} collective-permute-done((f32[4,4,64,1]{3,2,1,0:T(8,128)S(1)}, f32[4,4,64,1]{3,2,1,0:T(8,128)S(1)}, u32[]{:S(2)}, u32[]{:S(2)}) %collective-permute-start.3) | collective-permute-done | bytes 4128 | tf_op jit(solution)/shard_map/ppermute | solution.py:26
  29.9 0.5 select_maximum_fusion.4
  30.4 0.5 fusion.29
  30.9 0.2 fusion.2
  31.2 0.5 fusion.30
  31.7 0.0 copy-start.4
  31.7 0.3 fusion.1
  32.0 0.5 copy-done.4
  32.5 0.0 copy-done.9
  32.6 0.5 fusion.41
  33.0 0.1 maximum_bitcast_fusion.1
  33.1 0.9 copy-done
  34.1 1.2 multiply_reduce_fusion.1
  35.2 0.7 copy-done.2
  35.9 0.7 fusion.67
  36.7 4.7 %collective-permute-start.4 = (f32[4,1,64,128]{3,2,1,0:T(8,128)}, f32[4,1,64,128]{3,2,1,0:T(8,128)}, u32[]{:S(2)}, u32[]{:S(2)}) collective-permute-start(f32[4,1,64,128]{3,2,1,0:T(8,128)} %get-tuple-element.26), channel_id=1, source_target_pairs={{0,4},{4,8},{8,12},{12,16},{16,20},{20,24},{24,28},{1,5},{5,9},{9,... | collective-permute-start | bytes 393224 | tf_op jit(solution)/shard_map/ppermute | solution.py:23
  41.3 1.3 collective-permute-start.5
  42.6 36.5 %all-reduce.3 = (f32[4]{0:T(128)}, f32[4]{0:T(128)}) all-reduce(f32[4]{0:T(128)} %get-tuple-element.3, f32[4]{0:T(128)} %get-tuple-element.2), channel_id=1, replica_groups=mesh['gx'=2,'gy'=4,'gz'=4] {'gy','gz'}, use_global_device_ids=true, to_apply=%region_4.5 | all-reduce | flops 8 | bytes 64 | tf_op jit(solution)/shard_map/psum | solution.py:14
  79.1 5.6 %all-reduce.5 = (f32[4]{0:T(128)}, f32[4]{0:T(128)}) all-reduce(f32[4]{0:T(128)} %get-tuple-element.8, f32[4]{0:T(128)} %get-tuple-element.9), channel_id=1, replica_groups=mesh['gx'=2,'gy'=4,'gz'=4] {'gx'}, use_global_device_ids=true, to_apply=%region_5.6 | all-reduce | flops 8 | bytes 64 | tf_op jit(solution)/shard_map/psum | solution.py:15
  84.7 0.0 collective-permute-done.4
  84.7 0.0 collective-permute-done.5
  84.7 1.1 pad_maximum_fusion.2
  85.9 0.2 fusion.65
  86.1 2.6 %collective-permute-start.6 = (f32[4,4,64,1]{3,2,1,0:T(8,128)S(1)}, f32[4,4,64,1]{3,2,1,0:T(8,128)S(1)}, u32[]{:S(2)}, u32[]{:S(2)}) collective-permute-start(f32[4,4,64,1]{3,2,1,0:T(8,128)S(1)} %get-tuple-element.21), channel_id=1, source_target_pairs={{0,1},{1,2},{2,3},{4,5},{5,6},{6,7},{8,9},{9,10},{10,11},{12,13},{... | collective-permute-start | bytes 12296 | tf_op jit(solution)/shard_map/ppermute | solution.py:23
  88.7 1.3 collective-permute-start.7
  90.1 5.5 %collective-permute-done.6 = f32[4,4,64,1]{3,2,1,0:T(8,128)S(1)} collective-permute-done((f32[4,4,64,1]{3,2,1,0:T(8,128)S(1)}, f32[4,4,64,1]{3,2,1,0:T(8,128)S(1)}, u32[]{:S(2)}, u32[]{:S(2)}) %collective-permute-start.6) | collective-permute-done | bytes 4128 | tf_op jit(solution)/shard_map/ppermute | solution.py:23
  95.6 4.2 %collective-permute-done.7 = f32[4,4,64,1]{3,2,1,0:T(8,128)S(1)} collective-permute-done((f32[4,4,64,1]{3,2,1,0:T(8,128)S(1)}, f32[4,4,64,1]{3,2,1,0:T(8,128)S(1)}, u32[]{:S(2)}, u32[]{:S(2)}) %collective-permute-start.7) | collective-permute-done | bytes 4128 | tf_op jit(solution)/shard_map/ppermute | solution.py:26
  99.8 1.5 %select_maximum_fusion = f32[4,4,66,130]{3,2,1,0:T(8,128)S(1)} fusion(f32[4,4,64,1]{3,2,1,0:T(8,128)S(1)} %collective-permute-done.7, f32[4,4,64,1]{3,2,1,0:T(8,128)S(1)} %collective-permute-done.6, f32[4,1,64,128]{3,2,1,0:T(8,128)} %collective-permute-done.5, f32[4,2,64,128]{3,2,1,0:T(8,128)S(1)} %copy-done.3, f32[4,1,64,128]{3,2,1,0:T(8,128)} %collective-permute-done.4), kind=kLoop, calls=%fused_computation.8 | loop fusion | flops 1647360 | bytes 1081600 | tf_op jit(solution)/shard_map/concatenate | solution.py:27
  101.3 0.0 copy-done.15
  101.3 0.4 fusion.16
  101.8 0.0 copy-start.7
  101.8 0.4 fusion
  102.2 0.5 copy-done.7
  102.7 0.5 fusion.9
  103.2 0.0 copy-start.5
  103.2 0.5 broadcast_multiply_fusion
  103.7 1.2 copy-done.1
  104.9 0.8 fusion.35
  105.7 0.1 maximum_bitcast_fusion
  105.8 0.2 multiply_reduce_fusion
  106.0 0.9 copy.8
  106.9 3.4 %all-to-all-start = ((f32[4,2,64,128]{3,1,0,2:T(2,128)}), f32[4,2,64,128]{3,1,0,2:T(2,128)S(1)}, u32[]{:S(2)}, u32[]{:S(2)}) async-start(f32[4,2,64,128]{3,1,0,2:T(2,128)} %copy.8), calls=%async_computation | async-start | bytes 524288 | tf_op jit(solution)/shard_map/all_to_all | solution.py:100
  110.3 31.4 %all-reduce.2 = (f32[4]{0:T(128)S(1)}, f32[4]{0:T(128)S(1)}) all-reduce(f32[4]{0:T(128)S(1)} %get-tuple-element.5, f32[4]{0:T(128)S(1)} %get-tuple-element.4), channel_id=1, replica_groups=mesh['gx'=2,'gy'=4,'gz'=4] {'gy','gz'}, use_global_device_ids=true, to_apply=%region_10.11 | all-reduce | flops 8 | bytes 64 | tf_op jit(solution)/shard_map/psum | solution.py:14
  141.7 4.9 %all-reduce.4 = (f32[4]{0:T(128)S(1)}, f32[4]{0:T(128)S(1)}) all-reduce(f32[4]{0:T(128)S(1)} %get-tuple-element.6, f32[4]{0:T(128)S(1)} %get-tuple-element.7), channel_id=1, replica_groups=mesh['gx'=2,'gy'=4,'gz'=4] {'gx'}, use_global_device_ids=true, to_apply=%region_11.12 | all-reduce | flops 8 | bytes 64 | tf_op jit(solution)/shard_map/psum | solution.py:15
  146.6 0.5 add_divide_fusion
  147.1 0.0 all-to-all-done
  147.1 0.1 copy.9
  147.2 0.7 copy.10
  (33 shorter events, 0.2 us)
Async XLA Ops:
  2.4 0.6 copy-start.8
  4.0 4.0 %collective-permute-start = (f32[4,1,64,128]{3,2,1,0:T(8,128)S(1)}, f32[4,1,64,128]{3,2,1,0:T(8,128)S(1)}, u32[]{:S(2)}, u32[]{:S(2)}) collective-permute-start(f32[4,1,64,128]{3,2,1,0:T(8,128)S(1)} %get-tuple-element.28), channel_id=1, source_target_pairs={{0,4},{4,8},{8,12},{12,16},{16,20},{20,24},{24,28},{1,5},{5,9},{9,... | collective-permute-start | bytes 393224 | tf_op jit(solution)/shard_map/ppermute | solution.py:23
  6.4 5.3 %collective-permute-start.1 = (f32[4,1,64,128]{3,2,1,0:T(8,128)S(1)}, f32[4,1,64,128]{3,2,1,0:T(8,128)S(1)}, u32[]{:S(2)}, u32[]{:S(2)}) collective-permute-start(f32[4,1,64,128]{3,2,1,0:T(8,128)S(1)} %get-tuple-element.29), channel_id=1, source_target_pairs={{4,0},{8,4},{12,8},{16,12},{20,16},{24,20},{28,24},{5,1},{9,5},{13... | collective-permute-start | bytes 393224 | tf_op jit(solution)/shard_map/ppermute | solution.py:26
  7.9 23.2 %copy-start.6 = (f32[3,65,129]{2,1,0:T(8,128)}, f32[3,65,129]{2,1,0:T(8,128)S(1)}, u32[]{:S(2)}) copy-start(f32[3,65,129]{2,1,0:T(8,128)S(1)} %and_convert_fusion) | copy-start | bytes 301864
  12.0 13.2 %collective-permute-start.2 = (f32[4,4,64,1]{3,2,1,0:T(8,128)S(1)}, f32[4,4,64,1]{3,2,1,0:T(8,128)S(1)}, u32[]{:S(2)}, u32[]{:S(2)}) collective-permute-start(f32[4,4,64,1]{3,2,1,0:T(8,128)S(1)} %get-tuple-element.23), channel_id=1, source_target_pairs={{0,1},{1,2},{2,3},{4,5},{5,6},{6,7},{8,9},{9,10},{10,11},{12,13},{... | collective-permute-start | bytes 12296 | tf_op jit(solution)/shard_map/ppermute | solution.py:23
  15.5 14.4 %collective-permute-start.3 = (f32[4,4,64,1]{3,2,1,0:T(8,128)S(1)}, f32[4,4,64,1]{3,2,1,0:T(8,128)S(1)}, u32[]{:S(2)}, u32[]{:S(2)}) collective-permute-start(f32[4,4,64,1]{3,2,1,0:T(8,128)S(1)} %get-tuple-element.24), channel_id=1, source_target_pairs={{1,0},{2,1},{3,2},{5,4},{6,5},{7,6},{9,8},{10,9},{11,10},{13,12},{... | collective-permute-start | bytes 12296 | tf_op jit(solution)/shard_map/ppermute | solution.py:26
  16.8 14.1 %copy-start.14 = (pred[65]{0:T(512)(128)(4,1)}, pred[65]{0:T(512)(128)(4,1)S(1)}, u32[]{:S(2)}) copy-start(pred[65]{0:T(512)(128)(4,1)S(1)} %fusion.62) | copy-start | bytes 199
  31.7 0.8 copy-start.4
  31.7 0.9 copy-start.9
  32.6 1.5 %copy-start = (f32[4,3,3,65,129]{4,3,2,0,1:T(8,128)}, f32[4,3,3,65,129]{4,3,2,0,1:T(8,128)S(1)}, u32[]{:S(2)}) copy-start(f32[4,3,3,65,129]{4,3,2,0,1:T(8,128)S(1)} %fusion.1) | copy-start | bytes 3622324
  34.1 2.6 %copy-start.11 = (f32[2,64,128]{2,1,0:T(8,128)}, f32[2,64,128]{2,1,0:T(8,128)S(1)}, u32[]{:S(2)}) copy-start(f32[2,64,128]{2,1,0:T(8,128)S(1)} %maximum_bitcast_fusion.1) | copy-start | bytes 196612
  34.1 55.9 %copy-start.13 = (s32[4]{0:T(128)S(1)}, s32[4]{0:T(128)}, u32[]{:S(2)}) copy-start(s32[4]{0:T(128)} %param.3) | copy-start | bytes 52
  35.2 0.7 copy-start.2
  36.7 48.0 %collective-permute-start.4 = (f32[4,1,64,128]{3,2,1,0:T(8,128)}, f32[4,1,64,128]{3,2,1,0:T(8,128)}, u32[]{:S(2)}, u32[]{:S(2)}) collective-permute-start(f32[4,1,64,128]{3,2,1,0:T(8,128)} %get-tuple-element.26), channel_id=1, source_target_pairs={{0,4},{4,8},{8,12},{12,16},{16,20},{20,24},{24,28},{1,5},{5,9},{9,... | collective-permute-start | bytes 393224 | tf_op jit(solution)/shard_map/ppermute | solution.py:23
  41.3 43.4 %collective-permute-start.5 = (f32[4,1,64,128]{3,2,1,0:T(8,128)}, f32[4,1,64,128]{3,2,1,0:T(8,128)}, u32[]{:S(2)}, u32[]{:S(2)}) collective-permute-start(f32[4,1,64,128]{3,2,1,0:T(8,128)} %get-tuple-element.27), channel_id=1, source_target_pairs={{4,0},{8,4},{12,8},{16,12},{20,16},{24,20},{28,24},{5,1},{9,5},{13... | collective-permute-start | bytes 393224 | tf_op jit(solution)/shard_map/ppermute | solution.py:26
  84.7 5.3 %copy-start.16 = (f32[4]{0:T(128)S(1)}, f32[4]{0:T(128)}, u32[]{:S(2)}) copy-start(f32[4]{0:T(128)} %get-tuple-element.12) | copy-start | bytes 52
  84.7 5.4 %copy-start.17 = (f32[4]{0:T(128)S(1)}, f32[4]{0:T(128)}, u32[]{:S(2)}) copy-start(f32[4]{0:T(128)} %get-tuple-element.13) | copy-start | bytes 52
  84.7 15.1 %copy-start.3 = (f32[4,2,64,128]{3,2,1,0:T(8,128)S(1)}, f32[4,2,64,128]{3,2,1,0:T(8,128)}, u32[]{:S(2)}) copy-start(f32[4,2,64,128]{3,2,1,0:T(8,128)} %copy-done.2) | copy-start | bytes 786436
  85.8 15.5 %copy-start.15 = (pred[65]{0:T(512)(128)(4,1)S(1)}, pred[65]{0:T(512)(128)(4,1)}, u32[]{:S(2)}) copy-start(pred[65]{0:T(512)(128)(4,1)} %copy-done.14) | copy-start | bytes 199
  86.1 9.5 %collective-permute-start.6 = (f32[4,4,64,1]{3,2,1,0:T(8,128)S(1)}, f32[4,4,64,1]{3,2,1,0:T(8,128)S(1)}, u32[]{:S(2)}, u32[]{:S(2)}) collective-permute-start(f32[4,4,64,1]{3,2,1,0:T(8,128)S(1)} %get-tuple-element.21), channel_id=1, source_target_pairs={{0,1},{1,2},{2,3},{4,5},{5,6},{6,7},{8,9},{9,10},{10,11},{12,13},{... | collective-permute-start | bytes 12296 | tf_op jit(solution)/shard_map/ppermute | solution.py:23
  88.7 11.1 %collective-permute-start.7 = (f32[4,4,64,1]{3,2,1,0:T(8,128)S(1)}, f32[4,4,64,1]{3,2,1,0:T(8,128)S(1)}, u32[]{:S(2)}, u32[]{:S(2)}) collective-permute-start(f32[4,4,64,1]{3,2,1,0:T(8,128)S(1)} %get-tuple-element.22), channel_id=1, source_target_pairs={{1,0},{2,1},{3,2},{5,4},{6,5},{7,6},{9,8},{10,9},{11,10},{13,12},{... | collective-permute-start | bytes 12296 | tf_op jit(solution)/shard_map/ppermute | solution.py:26
  101.8 0.9 copy-start.7
  103.2 1.8 %copy-start.1 = (f32[4,3,3,65,129]{4,3,2,0,1:T(8,128)S(1)}, f32[4,3,3,65,129]{4,3,2,0,1:T(8,128)}, u32[]{:S(2)}) copy-start(f32[4,3,3,65,129]{4,3,2,0,1:T(8,128)} %copy-done) | copy-start | bytes 3622324
  103.2 1.7 %copy-start.5 = (f32[2,64,128]{2,1,0:T(8,128)S(1)}, f32[2,64,128]{2,1,0:T(8,128)}, u32[]{:S(2)}) copy-start(f32[2,64,128]{2,1,0:T(8,128)} %param.2) | copy-start | bytes 196612
  103.2 1.7 %copy-start.10 = (f32[2,64,128]{2,1,0:T(8,128)S(1)}, f32[2,64,128]{2,1,0:T(8,128)}, u32[]{:S(2)}) copy-start(f32[2,64,128]{2,1,0:T(8,128)} %copy-done.8) | copy-start | bytes 196612
  103.2 1.7 %copy-start.12 = (f32[2,64,128]{2,1,0:T(8,128)S(1)}, f32[2,64,128]{2,1,0:T(8,128)}, u32[]{:S(2)}) copy-start(f32[2,64,128]{2,1,0:T(8,128)} %copy-done.11) | copy-start | bytes 196612
  106.9 40.2 %all-to-all-start = ((f32[4,2,64,128]{3,1,0,2:T(2,128)}), f32[4,2,64,128]{3,1,0,2:T(2,128)S(1)}, u32[]{:S(2)}, u32[]{:S(2)}) async-start(f32[4,2,64,128]{3,1,0,2:T(2,128)} %copy.8), calls=%async_computation | async-start | bytes 524288 | tf_op jit(solution)/shard_map/all_to_all | solution.py:100
